TPU v7x, 512 devices: a whole 4x8x8 slice. The times are simulated.
512 devices in a mesh: probe: 4 (over x), seq: 128 (over y, z, core).
Axes of the slice: x: 4, y: 8, z: 8, core: 2. Of those that a mesh axis runs over, the one named last changes fastest.
Arguments:
- probe_bits: int32 [4, 128, 16384], P('probe', 'seq'), may hold values from 0 to 1
- noise_var: float32 [128, 16384], P('seq'), may hold values from 0.2 to 12
- kernel_spectrum: float32 [16384, 128], P('seq'), may hold values from 0.05 to 4, as said below
- symbol: float32 [16384, 128], P('seq'), may hold values from 0.3 to 3, as said below
- grad_prev: float32 [16384, 128], P('seq', 'probe'), may hold values from -6 to 6
Outputs:
- residual: float32 [4, 128, 16384], P('probe', 'seq')
- grad_total: float32 [16384, 128], P('seq', 'probe')
Inputs may be any that keep to these rules, and one draw needn't show every extreme that they name: kernel_spectrum at frequency k equals kernel_spectrum at frequency (2097152 - k) mod 2097152. symbol at frequency k equals symbol at frequency (2097152 - k) mod 2097152.
All inputs are finite; a program needn't handle non-finite values.
Results may differ from a plain program's by a relative error of at most 0.00017.
Values sent between devices are 32-bit elements; how exact they have to be, the bound alone decides.
A program may use at most 64 MiB of HBM per device.

v0:
```python
import math
import jax
import jax.numpy as jnp
from jax import lax
from jax.sharding import PartitionSpec as P

highest = lax.Precision.HIGHEST
minor_width = 128


def dft_table(height, breadth, modulus, orient):
    left_index = jnp.arange(height, dtype=jnp.int32)[:, None]
    right_index = jnp.arange(breadth, dtype=jnp.int32)[None, :]
    phases = (
        orient * 2.0 * math.pi / modulus * (left_index * right_index % modulus).astype(jnp.float32)
    )
    return (jnp.cos(phases), jnp.sin(phases))


def complex_product(pattern, real_part, imaginary, cosine_table, sine_table):
    real_cos = jnp.einsum(pattern, real_part, cosine_table, precision=highest)
    real_sin = jnp.einsum(pattern, real_part, sine_table, precision=highest)
    if imaginary is None:
        return (real_cos, real_sin)
    imag_cos = jnp.einsum(pattern, imaginary, cosine_table, precision=highest)
    imag_sin = jnp.einsum(pattern, imaginary, sine_table, precision=highest)
    return (real_cos - imag_sin, real_sin + imag_cos)


def rotate(real_part, imaginary, cosine_table, sine_table):
    return (
        real_part * cosine_table - imaginary * sine_table,
        real_part * sine_table + imaginary * cosine_table,
    )


def forward_rows(series):
    major_len = series.shape[-2]
    length = major_len * minor_width
    cosine_table, sine_table = dft_table(major_len, major_len, major_len, -1.0)
    section_real, section_imag = complex_product(
        "...mi,mk->...ik", series, None, cosine_table, sine_table
    )
    turn_cos, turn_sin = dft_table(minor_width, major_len, length, -1.0)
    twisted_real, twisted_imag = rotate(section_real, section_imag, turn_cos, turn_sin)
    cosine_table, sine_table = dft_table(minor_width, minor_width, minor_width, -1.0)
    return complex_product("...ik,ij->...jk", twisted_real, twisted_imag, cosine_table, sine_table)


def inverse_rows(real_part, imaginary):
    major_len = real_part.shape[-1]
    length = major_len * minor_width
    cosine_table, sine_table = dft_table(minor_width, minor_width, minor_width, 1.0)
    section_real, section_imag = complex_product(
        "...jk,ji->...ik", real_part, imaginary, cosine_table, sine_table
    )
    turn_cos, turn_sin = dft_table(minor_width, major_len, length, 1.0)
    twisted_real, twisted_imag = rotate(section_real, section_imag, turn_cos, turn_sin)
    cosine_table, sine_table = dft_table(major_len, major_len, major_len, 1.0)
    final_real, unused = complex_product(
        "...ik,km->...mi", twisted_real, twisted_imag, cosine_table, sine_table
    )
    return final_real


def global_twiddle(local_rows, major_len, samples, orient):
    row_index = lax.axis_index("seq") * local_rows + jnp.arange(local_rows, dtype=jnp.int32)
    column_index = (
        jnp.arange(minor_width, dtype=jnp.int32)[:, None] * major_len
        + jnp.arange(major_len, dtype=jnp.int32)[None, :]
    )
    phases = (
        orient
        * 2.0
        * math.pi
        / samples
        * (row_index[:, None, None] * column_index[None, :, :] % samples).astype(jnp.float32)
    )
    return (jnp.cos(phases), jnp.sin(phases))


def forward_spectrum(series):
    local_rows = series.shape[1]
    major_len = series.shape[2]
    devices = lax.axis_size("seq")
    all_rows = local_rows * devices
    samples = all_rows * major_len * minor_width
    real_part, imaginary = forward_rows(series)
    turn_cos, turn_sin = global_twiddle(local_rows, major_len, samples, -1.0)
    turned_real, turned_imag = rotate(real_part, imaginary, turn_cos, turn_sin)
    arrived = lax.all_to_all(
        jnp.stack([turned_real, turned_imag]), "seq", split_axis=3, concat_axis=2, tiled=True
    )
    block = minor_width // devices * major_len
    arrived = arrived.reshape(arrived.shape[0], arrived.shape[1], all_rows, block)
    cosine_table, sine_table = dft_table(all_rows, all_rows, all_rows, -1.0)
    return complex_product("zrb,ra->zba", arrived[0], arrived[1], cosine_table, sine_table)


def inverse_field(spectrum_real, spectrum_imag):
    all_rows = spectrum_real.shape[2]
    block = spectrum_real.shape[1]
    devices = lax.axis_size("seq")
    major_len = block * devices // minor_width
    cosine_table, sine_table = dft_table(all_rows, all_rows, all_rows, 1.0)
    back_real, back_imag = complex_product(
        "zba,ar->zrb", spectrum_real, spectrum_imag, cosine_table, sine_table
    )
    stacked = jnp.stack([back_real, back_imag])
    stacked = stacked.reshape(
        stacked.shape[0], stacked.shape[1], all_rows, minor_width // devices, major_len
    )
    arrived = lax.all_to_all(stacked, "seq", split_axis=2, concat_axis=3, tiled=True)
    local_rows = arrived.shape[2]
    samples = all_rows * major_len * minor_width
    turn_cos, turn_sin = global_twiddle(local_rows, major_len, samples, 1.0)
    turned_real, turned_imag = rotate(arrived[0], arrived[1], turn_cos, turn_sin)
    return inverse_rows(turned_real, turned_imag) / samples


def shards(probe_bits, noise_var, kernel_spectrum, symbol, grad_prev):
    field_shape = (
        probe_bits.shape[0],
        probe_bits.shape[1],
        probe_bits.shape[2] // minor_width,
        minor_width,
    )
    sign_field = (2 * probe_bits - 1).astype(jnp.float32).reshape(field_shape)
    noise_field = noise_var.reshape(field_shape[1:])
    samples = kernel_spectrum.shape[1] * noise_var.shape[1]
    base_real, base_imag = forward_spectrum(sign_field)
    scaled_real = base_real / symbol
    scaled_imag = base_imag / symbol
    precond = inverse_field(scaled_real, scaled_imag)
    again_real, again_imag = forward_spectrum(precond)
    circulant = inverse_field(kernel_spectrum * again_real, kernel_spectrum * again_imag)
    kernel_image = circulant + noise_field * precond
    numerator, curvature = lax.psum(
        (jnp.sum(sign_field * precond), jnp.sum(precond * kernel_image)), "seq"
    )
    step_size = numerator / curvature
    residual = sign_field - step_size * kernel_image
    cross_term = lax.psum(jnp.sum(residual * kernel_image), "seq")
    weight = -2.0 * cross_term
    resid_real, resid_imag = forward_spectrum(residual)
    applied = (
        inverse_field(kernel_spectrum * resid_real, kernel_spectrum * resid_imag)
        + noise_field * residual
    )
    adjoint = (
        weight / curvature * sign_field
        - 2.0 * weight * step_size / curvature * kernel_image
        - 2.0 * step_size * applied
    )
    adjoint_real, adjoint_imag = forward_spectrum(adjoint)
    local_grad = -(adjoint_real[0] * base_real[0] + adjoint_imag[0] * base_imag[0]) / (
        samples * symbol * symbol
    )
    probes = lax.axis_size("probe")
    summed = lax.psum(local_grad, "probe")
    share_width = summed.shape[1] // probes
    own_share = lax.dynamic_slice_in_dim(
        summed, lax.axis_index("probe") * share_width, share_width, 1
    )
    grad_total = grad_prev + own_share / probes
    return (residual.reshape(probe_bits.shape), grad_total)


def solution(mesh):
    placed = (
        P("probe", "seq", None),
        P("seq", None),
        P("seq", None),
        P("seq", None),
        P("seq", "probe"),
    )
    return jax.shard_map(
        shards,
        mesh=mesh,
        in_specs=placed,
        out_specs=(P("probe", "seq", None), P("seq", "probe")),
        check_vma=False,
    )
```

profile of v0, /device:TPU:8, one launch (start us, length us, event | category | flops | bytes accessed | tf_op | source)
XLA Modules:
  0.0 741.7 jit_solution(7742233880407343323)
XLA Ops:
  7.2 0.9 add_convert_fusion
  9.0 0.7 fusion.76
  9.7 0.7 fusion.64
  10.5 0.7 convolution_add_fusion.13
  11.2 0.9 subtract_bitcast_fusion.3
  12.2 29.0 %all_to_all.28 = f32[2,1,1,128,128]{4,2,1,0,3:T(1,128)S(1)} all-to-all(f32[2,1,1,128,128]{4,2,1,0,3:T(1,128)S(1)} %copy.13), channel_id=1, replica_groups=mesh['probe'=4,'seq'=128] {'seq'}, dimensions={3} | all-to-all | bytes 262144 | tf_op jit(solution)/shard_map/all_to_all | solution.py:91
  45.9 18.2 %all_to_all.29 = f32[2,1,128,1,128]{4,3,1,0,2:T(1,128)S(1)} all-to-all(f32[2,1,128,1,128]{4,3,1,0,2:T(1,128)S(1)} %copy.14), channel_id=1, replica_groups=mesh['probe'=4,'seq'=128] {'seq'}, dimensions={2} | all-to-all | bytes 262144 | tf_op jit(solution)/shard_map/all_to_all | solution.py:113
  64.1 0.7 fusion.82
  64.9 0.7 fusion.88
  65.6 0.7 convolution_subtract_fusion.13
  66.4 0.7 convolution_add_fusion.10
  67.1 0.8 fusion.43
  67.9 0.8 fusion.16
  69.6 0.7 fusion.61
  70.3 0.7 fusion.73
  71.0 0.7 convolution_add_fusion.9
  71.7 0.9 subtract_bitcast_fusion.2
  72.8 18.1 %all_to_all.30 = f32[2,1,1,128,128]{4,2,1,0,3:T(1,128)S(1)} all-to-all(f32[2,1,1,128,128]{4,2,1,0,3:T(1,128)S(1)} %copy.17), channel_id=1, replica_groups=mesh['probe'=4,'seq'=128] {'seq'}, dimensions={3} | all-to-all | bytes 262144 | tf_op jit(solution)/shard_map/all_to_all | solution.py:91
  95.5 17.8 %all_to_all.31 = f32[2,1,128,1,128]{4,3,1,0,2:T(1,128)S(1)} all-to-all(f32[2,1,128,1,128]{4,3,1,0,2:T(1,128)S(1)} %copy.18), channel_id=1, replica_groups=mesh['probe'=4,'seq'=128] {'seq'}, dimensions={2} | all-to-all | bytes 262144 | tf_op jit(solution)/shard_map/all_to_all | solution.py:113
  113.4 0.7 fusion.80
  114.1 0.7 fusion.86
  114.9 0.7 convolution_subtract_fusion.8
  115.6 0.7 convolution_add_fusion.6
  116.4 0.8 fusion.36
  117.2 1.4 multiply_reduce_fusion.1
  118.6 213.3 %all-reduce = (f32[]{:T(128)}, f32[]{:T(128)}) all-reduce(f32[]{:T(128)} %get-tuple-element.7, f32[]{:T(128)} %get-tuple-element.6), channel_id=1, replica_groups=mesh['probe'=4,'seq'=128] {'seq'}, use_global_device_ids=true, to_apply=%region_1.2 | all-reduce | flops 2 | bytes 16 | tf_op jit(solution)/shard_map/psum | solution.py:138
  334.8 0.7 fusion.58
  335.5 0.7 fusion.70
  336.3 0.7 convolution_add_fusion.5
  337.0 0.9 subtract_bitcast_fusion.1
  338.0 53.9 %all_to_all.32 = f32[2,1,1,128,128]{4,2,1,0,3:T(1,128)S(1)} all-to-all(f32[2,1,1,128,128]{4,2,1,0,3:T(1,128)S(1)} %copy.21), channel_id=1, replica_groups=mesh['probe'=4,'seq'=128] {'seq'}, dimensions={3} | all-to-all | bytes 262144 | tf_op jit(solution)/shard_map/all_to_all | solution.py:91
  396.0 0.8 copy.22
  396.8 6.6 all-to-all-start.5
  403.4 217.7 %psum.30 = f32[]{:T(128)} all-reduce(f32[]{:T(128)} %get-tuple-element.10), channel_id=1, replica_groups=mesh['probe'=4,'seq'=128] {'seq'}, use_global_device_ids=true, to_apply=%region_5.6 | all-reduce | flops 1 | bytes 8 | tf_op jit(solution)/shard_map/psum | solution.py:143
  623.9 0.7 fusion.78
  624.7 0.7 fusion.84
  625.4 0.7 convolution_subtract_fusion.3
  626.2 0.7 convolution_add_fusion.2
  626.9 0.8 fusion.29
  627.7 0.8 fusion.20
  629.4 0.7 fusion.55
  630.1 0.7 fusion.67
  630.8 0.7 convolution_add_fusion.1
  631.5 0.9 subtract_bitcast_fusion
  632.6 53.0 %all_to_all.33 = f32[2,1,1,128,128]{4,2,1,0,3:T(1,128)S(1)} all-to-all(f32[2,1,1,128,128]{4,2,1,0,3:T(1,128)S(1)} %copy.25), channel_id=1, replica_groups=mesh['probe'=4,'seq'=128] {'seq'}, dimensions={3} | all-to-all | bytes 262144 | tf_op jit(solution)/shard_map/all_to_all | solution.py:91
  687.1 1.1 fusion.21
  689.0 44.0 %all-reduce.3.cloned.1.call-done = f32[128,128]{1,0:T(8,128)} async-done(((f32[128,128]{1,0:T(8,128)}), f32[128,128]{1,0:T(8,128)}) %all-reduce.3.cloned.1.call-update) | async-done | bytes 65552 | tf_op jit(solution)/shard_map/psum | solution.py:160
  733.0 0.9 multiply_add_fusion
  (72 shorter events, 21.3 us)
Async XLA Ops:
  42.3 0.8 copy-start.4
  91.4 0.8 copy-start.2
  116.4 0.8 copy-start.3
  333.9 293.8 %copy-start = (f32[128,128]{1,0:T(8,128)}, f32[128,128]{1,0:T(8,128)S(1)}, u32[]{:S(2)}) copy-start(f32[128,128]{1,0:T(8,128)S(1)} %get-tuple-element.11) | copy-start | bytes 196612
  396.8 227.0 %all-to-all-start.5 = ((f32[2,1,128,1,128]{4,3,1,0,2:T(1,128)}), f32[2,1,128,1,128]{4,3,1,0,2:T(1,128)S(1)}, u32[]{:S(2)}, u32[]{:S(2)}) async-start(f32[2,1,128,1,128]{4,3,1,0,2:T(1,128)} %copy.22), calls=%async_computation.5 | async-start | bytes 262144 | tf_op jit(solution)/shard_map/all_to_all | solution.py:113
  403.4 329.7 %all-reduce.3.cloned.1.call-start = ((), (), s32[]{:S(2)}) async-start(), calls=%async_computation.7 | async-start | bytes 131072 | tf_op jit(solution)/shard_map/psum | solution.py:160
  688.2 0.7 copy-start.1
Sparse Core Ops, SparseCore 0:
  688.3 44.6 all-reduce.2
where the time goes:
time: 750 us; the launch traced here: 742 us
  blocking collectives  621 us (83%)
  waiting for transfers between devices  44.1 us (6%)
  matrix products  43.9 us (6%)
  between operations  18.9 us (3%)
    psum x1, blocking collectives, shards(): cross_term = lax.psum(jnp.sum(residual * kernel_image), 'seq')  218 us
    psum x1, blocking collectives, shards(): lax.psum((jnp.sum(sign_field * precond), jnp.sum(precond * kernel_image))...  213 us
    all_to_all x4, blocking collectives, forward_spectrum(): lax.all_to_all(jnp.stack([turned_real, turned_imag]), 'seq', split_axis=3...  154 us
    psum x1, waiting for transfers between devices, shards(): summed = lax.psum(local_grad, 'probe')  44 us
    all_to_all x2, blocking collectives, inverse_field(): lax.all_to_all(stacked, 'seq', split_axis=2, concat_axis=3, tiled=True)  36 us
  transfers between devices with their start and end apart: 2, of which 1 were waited for; matrix products, arithmetic and copies ran while one was open for 0% of the time, Pallas kernels for 0%

commit v1 on v0

--- a/solution.py
+++ b/solution.py
@@ -157,7 +157,9 @@
         samples * symbol * symbol
     )
     probes = lax.axis_size("probe")
-    summed = lax.psum(local_grad, "probe")
+    summed = local_grad
+    for hop in (1, 2):
+        summed = summed + lax.ppermute(summed, "probe", [(dev, dev ^ hop) for dev in range(4)])
     share_width = summed.shape[1] // probes
     own_share = lax.dynamic_slice_in_dim(
         summed, lax.axis_index("probe") * share_width, share_width, 1

time: 750 us -> 707 us (0.943)
  the two profiles are of different devices: /device:TPU:8 before, /device:TPU:4 now
where the time goes in v1:
time: 707 us; the launch traced here: 698 us
  blocking collectives  593 us (84%)
  matrix products  43.7 us (6%)
  starting transfers between devices  29.6 us (4%)
  waiting for transfers between devices  20.5 us (3%)
    psum x1, blocking collectives, shards(): cross_term = lax.psum(jnp.sum(residual * kernel_image), 'seq')  253 us
    psum x1, blocking collectives, shards(): lax.psum((jnp.sum(sign_field * precond), jnp.sum(precond * kernel_image))...  248 us
    all_to_all x3, blocking collectives, forward_spectrum(): lax.all_to_all(jnp.stack([turned_real, turned_imag]), 'seq', split_axis=3...  55.9 us
    all_to_all x2, blocking collectives, inverse_field(): lax.all_to_all(stacked, 'seq', split_axis=2, concat_axis=3, tiled=True)  35.9 us
    all_to_all x1, starting transfers between devices, forward_spectrum(): lax.all_to_all(jnp.stack([turned_real, turned_imag]), 'seq', split_axis=3...  17.9 us
  transfers between devices with their start and end apart: 4, of which 3 were waited for; matrix products, arithmetic and copies ran while one was open for 0% of the time, Pallas kernels for 0%

profile of v1, /device:TPU:4, one launch (start us, length us, event | category | flops | bytes accessed | tf_op | source)
XLA Modules:
  0.0 697.7 jit_solution(15943721043480661680)
XLA Ops:
  0.6 0.9 add_convert_fusion
  2.5 0.7 fusion.76
  3.2 0.7 fusion.64
  3.9 0.7 convolution_add_fusion.13
  4.6 0.9 subtract_bitcast_fusion.3
  5.5 0.8 copy.11
  6.3 17.9 %all-to-all-start = ((f32[2,1,1,128,128]{4,2,1,0,3:T(1,128)}), f32[2,1,1,128,128]{4,2,1,0,3:T(1,128)S(1)}, u32[]{:S(2)}, u32[]{:S(2)}) async-start(f32[2,1,1,128,128]{4,2,1,0,3:T(1,128)} %copy.11), calls=%async_computation | async-start | bytes 262144 | tf_op jit(solution)/shard_map/all_to_all | solution.py:91
  24.4 12.2 %all-to-all-done = f32[2,1,1,128,128]{4,2,1,0,3:T(1,128)S(1)} async-done(((f32[2,1,1,128,128]{4,2,1,0,3:T(1,128)}), f32[2,1,1,128,128]{4,2,1,0,3:T(1,128)S(1)}, u32[]{:S(2)}, u32[]{:S(2)}) %all-to-all-start) | async-done | bytes 131104 | tf_op jit(solution)/shard_map/all_to_all | solution.py:91
  41.1 18.1 %all_to_all.28 = f32[2,1,128,1,128]{4,3,1,0,2:T(1,128)S(1)} all-to-all(f32[2,1,128,1,128]{4,3,1,0,2:T(1,128)S(1)} %copy.14), channel_id=1, replica_groups=mesh['probe'=4,'seq'=128] {'seq'}, dimensions={2} | all-to-all | bytes 262144 | tf_op jit(solution)/shard_map/all_to_all | solution.py:113
  59.2 0.7 fusion.88
  60.0 0.7 fusion.82
  60.7 0.7 convolution_add_fusion.10
  61.5 0.7 convolution_subtract_fusion.13
  62.2 0.8 fusion.43
  63.0 0.8 fusion.16
  64.7 0.7 fusion.73
  66.1 0.7 convolution_add_fusion.9
  66.8 0.9 subtract_bitcast_fusion.2
  67.9 18.1 %all_to_all.29 = f32[2,1,1,128,128]{4,2,1,0,3:T(1,128)S(1)} all-to-all(f32[2,1,1,128,128]{4,2,1,0,3:T(1,128)S(1)} %copy.17), channel_id=1, replica_groups=mesh['probe'=4,'seq'=128] {'seq'}, dimensions={3} | all-to-all | bytes 262144 | tf_op jit(solution)/shard_map/all_to_all | solution.py:91
  90.6 17.8 %all_to_all.30 = f32[2,1,128,1,128]{4,3,1,0,2:T(1,128)S(1)} all-to-all(f32[2,1,128,1,128]{4,3,1,0,2:T(1,128)S(1)} %copy.18), channel_id=1, replica_groups=mesh['probe'=4,'seq'=128] {'seq'}, dimensions={2} | all-to-all | bytes 262144 | tf_op jit(solution)/shard_map/all_to_all | solution.py:113
  108.5 0.7 fusion.86
  109.3 0.7 fusion.80
  110.0 0.7 convolution_add_fusion.6
  110.7 0.7 convolution_subtract_fusion.8
  111.5 0.8 fusion.36
  112.3 1.4 multiply_reduce_fusion.1
  113.7 248.0 %all-reduce = (f32[]{:T(128)}, f32[]{:T(128)}) all-reduce(f32[]{:T(128)} %get-tuple-element.3, f32[]{:T(128)} %get-tuple-element.2), channel_id=1, replica_groups=mesh['probe'=4,'seq'=128] {'seq'}, use_global_device_ids=true, to_apply=%region_1.2 | all-reduce | flops 2 | bytes 16 | tf_op jit(solution)/shard_map/psum | solution.py:138
  364.6 0.7 fusion.70
  365.3 0.7 fusion.58
  366.1 0.7 convolution_add_fusion.5
  366.8 0.9 subtract_bitcast_fusion.1
  367.8 19.3 %all_to_all.31 = f32[2,1,1,128,128]{4,2,1,0,3:T(1,128)S(1)} all-to-all(f32[2,1,1,128,128]{4,2,1,0,3:T(1,128)S(1)} %copy.21), channel_id=1, replica_groups=mesh['probe'=4,'seq'=128] {'seq'}, dimensions={3} | all-to-all | bytes 262144 | tf_op jit(solution)/shard_map/all_to_all | solution.py:91
  391.2 0.8 copy.22
  392.0 6.1 all-to-all-start.5
  398.1 252.8 %psum.23 = f32[]{:T(128)} all-reduce(f32[]{:T(128)} %get-tuple-element.6), channel_id=1, replica_groups=mesh['probe'=4,'seq'=128] {'seq'}, use_global_device_ids=true, to_apply=%region_5.6 | all-reduce | flops 1 | bytes 8 | tf_op jit(solution)/shard_map/psum | solution.py:143
  653.8 0.7 fusion.84
  654.5 0.7 fusion.78
  655.3 0.7 convolution_add_fusion.2
  656.0 0.7 convolution_subtract_fusion.3
  656.8 0.8 fusion.29
  657.5 0.8 fusion.20
  660.7 0.7 convolution_add_fusion.1
  661.4 0.9 subtract_bitcast_fusion
  662.4 18.5 %all_to_all.32 = f32[2,1,1,128,128]{4,2,1,0,3:T(1,128)S(1)} all-to-all(f32[2,1,1,128,128]{4,2,1,0,3:T(1,128)S(1)} %copy.25), channel_id=1, replica_groups=mesh['probe'=4,'seq'=128] {'seq'}, dimensions={3} | all-to-all | bytes 262144 | tf_op jit(solution)/shard_map/all_to_all | solution.py:91
  683.1 3.1 collective-permute-start
  686.2 3.0 collective-permute-done
  689.3 2.4 collective-permute-start.1
  691.7 5.2 collective-permute-done.1
  (74 shorter events, 23.1 us)
Async XLA Ops:
  6.3 18.0 %copy-start.1 = (f32[128,128]{1,0:T(8,128)S(1)}, f32[128,128]{1,0:T(8,128)}, u32[]{:S(2)}) copy-start(f32[128,128]{1,0:T(8,128)} %param.8) | copy-start | bytes 196612
  6.3 30.3 %all-to-all-start = ((f32[2,1,1,128,128]{4,2,1,0,3:T(1,128)}), f32[2,1,1,128,128]{4,2,1,0,3:T(1,128)S(1)}, u32[]{:S(2)}, u32[]{:S(2)}) async-start(f32[2,1,1,128,128]{4,2,1,0,3:T(1,128)} %copy.11), calls=%async_computation | async-start | bytes 262144 | tf_op jit(solution)/shard_map/all_to_all | solution.py:91
  86.5 0.8 copy-start.3
  111.5 0.8 copy-start.4
  363.7 293.8 %copy-start = (f32[128,128]{1,0:T(8,128)}, f32[128,128]{1,0:T(8,128)S(1)}, u32[]{:S(2)}) copy-start(f32[128,128]{1,0:T(8,128)S(1)} %get-tuple-element.7) | copy-start | bytes 196612
  392.0 261.7 %all-to-all-start.5 = ((f32[2,1,128,1,128]{4,3,1,0,2:T(1,128)}), f32[2,1,128,1,128]{4,3,1,0,2:T(1,128)S(1)}, u32[]{:S(2)}, u32[]{:S(2)}) async-start(f32[2,1,128,1,128]{4,3,1,0,2:T(1,128)} %copy.22), calls=%async_computation.5 | async-start | bytes 262144 | tf_op jit(solution)/shard_map/all_to_all | solution.py:113
  683.1 6.2 collective-permute-start
  689.3 7.7 %copy-start.2 = (f32[128,32]{0,1:T(8,128)S(1)}, f32[128,32]{0,1:T(8,128)}, u32[]{:S(2)}) copy-start(f32[128,32]{0,1:T(8,128)} %param.9) | copy-start | bytes 49156
  689.3 7.7 %collective-permute-start.1 = (f32[128,128]{0,1:T(8,128)S(1)}, f32[128,128]{0,1:T(8,128)S(1)}, u32[]{:S(2)}, u32[]{:S(2)}) collective-permute-start(f32[128,128]{0,1:T(8,128)S(1)} %add.649), channel_id=1, source_target_pairs={{0,256},{128,384},{256,0},{384,128},{1,257},{129,385},{257,1},{385... | collective-permute-start | bytes 196616 | tf_op jit(solution)/shard_map/ppermute | solution.py:162
